TPU v7x, 32 devices: a whole 2x2x4 slice. The times are simulated.
32 devices in a mesh: row: 4 (over y, core), col: 8 (over z, x).
Axes of the slice: x: 2, y: 2, z: 4, core: 2. Of those that a mesh axis runs over, the one named last changes fastest.
Arguments:
- inner_base: bfloat16 [4, 1, 2, 4096, 14336], P(None, None, None, 'row', 'col'), may hold values from -250 to 250
- inner_left: bfloat16 [4, 1, 2, 4096, 16], P(None, None, None, ('row', 'col')), may hold values from -6 to 6
- inner_right: bfloat16 [4, 1, 2, 16, 14336], P(None, None, None, 'row', 'col'), may hold values from -12 to 12
- inner_mag: float32 [4, 1, 2, 14336], P(None, None, None, 'col'), may hold values from 512 to 2048
- outer_base: bfloat16 [4, 1, 14336, 4096], P(None, None, 'row', 'col'), may hold values from -250 to 250
- outer_left: bfloat16 [4, 1, 14336, 16], P(None, None, ('row', 'col')), may hold values from -6 to 6
- outer_right: bfloat16 [4, 1, 16, 4096], P(None, None, 'row', 'col'), may hold values from -12 to 12
- outer_mag: float32 [4, 1, 4096], P(None, None, 'col'), may hold values from 1792 to 7168
Outputs:
- inner_merged: bfloat16 [4, 1, 2, 4096, 14336], P(None, None, None, 'row', 'col')
- outer_merged: bfloat16 [4, 1, 14336, 4096], P(None, None, 'row', 'col')
All inputs are finite; a program needn't handle non-finite values.
Results may differ from a plain program's by a relative error of at most 0.001.
Values may be sent and summed in bfloat16 or wider, within the bound.
A program may use at most 256 MiB of HBM per device.

v0:
```python
import jax
import jax.numpy as jnp
from jax import lax
from jax.sharding import PartitionSpec as P

epsilon = 1e-06


def combine_tile(base, left, right):
    delta = jnp.einsum("...ik,...kj->...ij", left, right, preferred_element_type=jnp.float32)
    return base.astype(jnp.float32) + delta


def merge_layer(
    inner_base, outer_base, inner_mag, outer_mag, inner_left, outer_left, inner_right, outer_right
):
    inner_full = combine_tile(inner_base, inner_left, inner_right)
    outer_full = combine_tile(outer_base, outer_left, outer_right)
    inner_squares = jnp.sum(inner_full * inner_full, axis=-2)
    outer_squares = jnp.sum(outer_full * outer_full, axis=-2)
    inner_totals, outer_totals = lax.psum((inner_squares, outer_squares), "row")
    inner_scale = lax.rsqrt(inner_totals + epsilon)
    outer_scale = lax.rsqrt(outer_totals + epsilon)
    inner_factor = inner_mag * inner_scale
    outer_factor = outer_mag * outer_scale
    inner_merged = (inner_factor[..., None, :] * inner_full).astype(jnp.bfloat16)
    outer_merged = (outer_factor[..., None, :] * outer_full).astype(jnp.bfloat16)
    return (inner_merged, outer_merged)


def shards(
    inner_base, inner_left, inner_right, inner_mag, outer_base, outer_left, outer_right, outer_mag
):
    layer_count = inner_base.shape[0]
    inner_outputs = []
    outer_outputs = []
    inner_rows, outer_rows = (
        lax.all_gather(inner_left, "col", axis=3, tiled=True),
        lax.all_gather(outer_left, "col", axis=2, tiled=True),
    )
    inner_ranks, outer_ranks = (
        lax.all_gather(inner_right, "row", axis=3, tiled=True),
        lax.all_gather(outer_right, "row", axis=2, tiled=True),
    )
    for layer_index in range(layer_count):
        inner_merged, outer_merged = merge_layer(
            inner_base[layer_index],
            outer_base[layer_index],
            inner_mag[layer_index],
            outer_mag[layer_index],
            inner_rows[layer_index],
            outer_rows[layer_index],
            inner_ranks[layer_index],
            outer_ranks[layer_index],
        )
        inner_outputs.append(inner_merged)
        outer_outputs.append(outer_merged)
    return (jnp.stack(inner_outputs), jnp.stack(outer_outputs))


def solution(mesh):
    in_specs = (
        P(None, None, None, "row", "col"),
        P(None, None, None, ("row", "col"), None),
        P(None, None, None, "row", "col"),
        P(None, None, None, "col"),
        P(None, None, "row", "col"),
        P(None, None, ("row", "col"), None),
        P(None, None, "row", "col"),
        P(None, None, "col"),
    )
    out_specs = (P(None, None, None, "row", "col"), P(None, None, "row", "col"))
    return jax.shard_map(shards, mesh=mesh, in_specs=in_specs, out_specs=out_specs, check_vma=False)
```

profile of v0, /device:TPU:0, one launch (start us, length us, event | category | flops | bytes accessed | tf_op | source)
XLA Modules:
  0.0 347.4 jit_solution(11478895397710720571)
XLA Ops:
  7.2 0.9 copy.17
  8.2 8.3 %all_gather.13 = bf16[4,1,2,16,1792]{4,0,2,1,3:T(4,128)(2,1)S(1)} all-gather(bf16[4,1,2,4,1792]{4,0,2,1,3:T(4,128)(2,1)S(1)} %copy.17), channel_id=1, replica_groups=mesh['row'=4,'col'=8] {'row'}, dimensions={3}, use_global_device_ids=true | all-gather | bytes 573440 | tf_op jit(solution)/shard_map/all_gather | solution.py:42
  17.1 27.0 %all_gather.12 = bf16[4,1,2,1024,16]{3,4,2,1,0:T(8,128)(2,1)S(1)} all-gather(bf16[4,1,2,128,16]{3,4,2,1,0:T(8,128)(2,1)} %param.9), channel_id=1, replica_groups=mesh['row'=4,'col'=8] {'col'}, dimensions={3}, use_global_device_ids=true | all-gather | bytes 294912 | tf_op jit(solution)/shard_map/all_gather | solution.py:38
  44.1 7.6 %fusion.10 = f32[2,1024,1792]{2,1,0:T(8,128)} fusion(bf16[1,1,2,16,1792]{4,0,2,1,3:T(2,128)(2,1)S(1)} %get-tuple-element.23, bf16[4,1,2,1024,16]{3,4,2,1,0:T(8,128)(2,1)S(1)} %all_gather.12), kind=kOutput, calls=%fused_computation.39 | convolution fusion | flops 117440512 | bytes 14974976 | tf_op jit(solution)/shard_map/...ik,...kj->...ij/dot_general | solution.py:10
  51.7 7.3 %fusion.8 = f32[2,1024,1792]{2,1,0:T(8,128)} fusion(bf16[1,1,2,16,1792]{4,0,2,1,3:T(2,128)(2,1)S(1)} %get-tuple-element.25, bf16[4,1,2,1024,16]{3,4,2,1,0:T(8,128)(2,1)S(1)} %all_gather.12), kind=kOutput, calls=%fused_computation.35 | convolution fusion | flops 117440512 | bytes 14974976 | tf_op jit(solution)/shard_map/...ik,...kj->...ij/dot_general | solution.py:10
  59.0 7.3 %fusion.9 = f32[2,1024,1792]{2,1,0:T(8,128)} fusion(bf16[1,1,2,16,1792]{4,0,2,1,3:T(2,128)(2,1)S(1)} %get-tuple-element.22, bf16[4,1,2,1024,16]{3,4,2,1,0:T(8,128)(2,1)S(1)} %all_gather.12), kind=kOutput, calls=%fused_computation.37 | convolution fusion | flops 117440512 | bytes 14974976 | tf_op jit(solution)/shard_map/...ik,...kj->...ij/dot_general | solution.py:10
  66.6 69.6 %all_gather.14 = bf16[4,1,3584,16]{3,0,1,2:T(4,128)(2,1)S(1)} all-gather(bf16[4,1,448,16]{3,0,1,2:T(4,128)(2,1)S(1)} %copy.22), channel_id=1, replica_groups=mesh['row'=4,'col'=8] {'col'}, dimensions={2}, use_global_device_ids=true | all-gather | bytes 516096 | tf_op jit(solution)/shard_map/all_gather | solution.py:39
  136.2 6.7 %fusion.20 = (bf16[1,1,3584,16]{3,0,1,2:T(2,128)(2,1)}, bf16[1,1,3584,16]{3,0,1,2:T(2,128)(2,1)}, bf16[1,1,3584,16]{3,0,1,2:T(2,128)(2,1)}, bf16[1,1,3584,16]{3,0,1,2:T(2,128)(2,1)S(1)}) fusion(bf16[4,1,3584,16]{3,0,1,2:T(4,128)(2,1)S(1)} %all_gather.14), kind=kLoop, calls=%fused_computation.66 | loop fusion | bytes 917504 | tf_op jit(solution)/shard_map/slice | solution.py:52
  142.9 3.5 %copy.36 = bf16[1,1,3584,16]{2,3,1,0:T(8,128)(2,1)S(1)} copy(bf16[1,1,3584,16]{3,0,1,2:T(2,128)(2,1)} %get-tuple-element.18) | data formatting | bytes 229376
  146.4 5.2 %all_gather.15 = bf16[4,1,16,512]{3,0,1,2:T(4,128)(2,1)S(1)} all-gather(bf16[4,1,4,512]{3,0,1,2:T(4,128)(2,1)S(1)} %copy.24), channel_id=1, replica_groups=mesh['row'=4,'col'=8] {'row'}, dimensions={2}, use_global_device_ids=true | all-gather | bytes 81920 | tf_op jit(solution)/shard_map/all_gather | solution.py:43
  151.8 3.7 %copy.38 = bf16[1,1,3584,16]{2,3,1,0:T(8,128)(2,1)S(1)} copy(bf16[1,1,3584,16]{3,0,1,2:T(2,128)(2,1)} %get-tuple-element.20) | data formatting | bytes 229376
  155.5 3.5 %copy.40 = bf16[1,1,3584,16]{2,3,1,0:T(8,128)(2,1)S(1)} copy(bf16[1,1,3584,16]{3,0,1,2:T(2,128)(2,1)} %get-tuple-element.19) | data formatting | bytes 229376
  159.0 1.8 copy.42
  160.8 6.7 %multiply_reduce_fusion.7 = (f32[512]{0:T(512)}, f32[3584,512]{1,0:T(8,128)}) fusion(bf16[1,1,16,512]{3,0,1,2:T(2,128)(2,1)S(1)} %get-tuple-element.26, bf16[1,1,3584,16]{2,3,1,0:T(8,128)(2,1)S(1)} %copy.36, bf16[4,1,3584,512]{3,2,1,0:T(8,128)(2,1)} %param.12), kind=kOutput, calls=%fused_computation.29 | convolution fusion | flops 66059776 | bytes 11143168 | tf_op jit(solution)/shard_map/...ik,...kj->...ij/dot_general | solution.py:10
  167.5 6.8 %multiply_reduce_fusion.6 = (f32[512]{0:T(512)}, f32[3584,512]{1,0:T(8,128)}) fusion(bf16[1,1,16,512]{3,0,1,2:T(2,128)(2,1)S(1)} %get-tuple-element.28, bf16[1,1,3584,16]{2,3,1,0:T(8,128)(2,1)S(1)} %copy.38, bf16[4,1,3584,512]{3,2,1,0:T(8,128)(2,1)} %param.12), kind=kOutput, calls=%fused_computation.27 | convolution fusion | flops 66059776 | bytes 11143168 | tf_op jit(solution)/shard_map/...ik,...kj->...ij/dot_general | solution.py:10
  174.3 6.8 %multiply_reduce_fusion.5 = (f32[512]{0:T(512)}, f32[3584,512]{1,0:T(8,128)}) fusion(bf16[1,1,16,512]{3,0,1,2:T(2,128)(2,1)S(1)} %get-tuple-element.27, bf16[1,1,3584,16]{2,3,1,0:T(8,128)(2,1)S(1)} %copy.40, bf16[4,1,3584,512]{3,2,1,0:T(8,128)(2,1)} %param.12), kind=kOutput, calls=%fused_computation.25 | convolution fusion | flops 66059776 | bytes 11143168 | tf_op jit(solution)/shard_map/...ik,...kj->...ij/dot_general | solution.py:10
  181.0 6.8 %multiply_reduce_fusion.4 = (f32[512]{0:T(512)}, f32[3584,512]{1,0:T(8,128)}) fusion(bf16[1,1,16,512]{3,0,1,2:T(2,128)(2,1)S(1)} %get-tuple-element.29, bf16[1,1,3584,16]{2,3,1,0:T(8,128)(2,1)S(1)} %copy.42, bf16[4,1,3584,512]{3,2,1,0:T(8,128)(2,1)} %param.12), kind=kOutput, calls=%fused_computation.23 | convolution fusion | flops 66059776 | bytes 11143168 | tf_op jit(solution)/shard_map/...ik,...kj->...ij/dot_general | solution.py:10
  187.8 30.8 %multiply_reduce_fusion.3 = (f32[2,1792]{1,0:T(2,128)}, f32[2,1792]{1,0:T(2,128)}, f32[2,1792]{1,0:T(2,128)}, f32[2,1792]{1,0:T(2,128)}, f32[2,1024,1792]{2,1,0:T(8,128)}) fusion(bf16[4,1,2,1024,1792]{4,3,2,1,0:T(8,128)(2,1)} %param.8, f32[2,1024,1792]{2,1,0:T(8,128)} %fusion.10, f32[2,1024,1792]{2,1,0:T(8,128)} %fusion.8, f32[2,1024,1792]{2,1,0:T(8,128)} %fusion.9, ...), kind=kOutput, calls=%fused_computation.13 | convolution fusion | flops 176146432 | bytes 88432640 | tf_op jit(solution)/shard_map/...ik,...kj->...ij/dot_general | solution.py:10
  218.6 30.6 %all-reduce.3.cloned.1.call-done = (f32[1,2,1792]{2,1,0:T(2,128)}, f32[1,2,1792]{2,1,0:T(2,128)}, f32[1,2,1792]{2,1,0:T(2,128)}, f32[1,2,1792]{2,1,0:T(2,128)}, ...) async-done(((f32[1,2,1792]{2,1,0:T(2,128)}, f32[1,2,1792]{2,1,0:T(2,128)}, f32[1,2,1792]{2,1,0:T(2,128)}, f32[1,2,1792]{2,1,0:T(2,128)}, ...) | async-done | bytes 65552 | tf_op jit(solution)/shard_map/psum | solution.py:21
  249.9 9.1 %fusion.4 = (bf16[1,1,3584,512]{3,2,1,0:T(8,128)(2,1)S(1)}, bf16[1,1,3584,512]{3,2,1,0:T(8,128)(2,1)}) fusion(f32[3584,512]{1,0:T(8,128)} %get-tuple-element.46, f32[512]{0:T(512)S(1)} %bitcast.166, f32[3584,512]{1,0:T(8,128)} %get-tuple-element.44, f32[512]{0:T(512)S(1)} %bitcast.167), kind=kLoop, calls=%fused_computation.30 | loop fusion | flops 7340032 | bytes 22024192 | tf_op jit(solution)/shard_map/stack | solution.py:58
  259.0 10.2 %fusion.6 = (bf16[1,1,3584,512]{3,2,1,0:T(8,128)(2,1)}, bf16[1,1,3584,512]{3,2,1,0:T(8,128)(2,1)}) fusion(f32[3584,512]{1,0:T(8,128)} %get-tuple-element.42, f32[512]{0:T(512)S(1)} %bitcast.165, f32[3584,512]{1,0:T(8,128)} %get-tuple-element.40, f32[512]{0:T(512)S(1)} %bitcast.164), kind=kLoop, calls=%fused_computation.32 | loop fusion | flops 7340032 | bytes 22024192 | tf_op jit(solution)/shard_map/stack | solution.py:58
  269.3 11.8 %pad_maximum_fusion.1 = bf16[4,1,3584,512]{3,2,1,0:T(8,128)(2,1)} fusion(bf16[1,1,3584,512]{3,2,1,0:T(8,128)(2,1)} %get-tuple-element.50, bf16[1,1,3584,512]{3,2,1,0:T(8,128)(2,1)} %get-tuple-element.49, bf16[1,1,3584,512]{3,2,1,0:T(8,128)(2,1)} %get-tuple-element.48, bf16[1,1,3584,512]{3,2,1,0:T(8,128)(2,1)S(1)} %get-tuple-element.47), kind=kLoop, calls=%fused_computation.1 | loop fusion | flops 22020096 | bytes 29360128 | tf_op jit(solution)/shard_map/stack | solution.py:58
  281.2 38.7 %fusion = (bf16[1,1,2,1024,1792]{4,3,2,1,0:T(8,128)(2,1)}, bf16[1,1,2,1024,1792]{4,3,2,1,0:T(8,128)(2,1)}, bf16[1,1,2,1024,1792]{4,3,2,1,0:T(8,128)(2,1)}, bf16[1,1,2,1024,1792]{4,3,2,1,0:T(8,128)(2,1)}) fusion(f32[2,1024,1792]{2,1,0:T(8,128)} %get-tuple-element.38, f32[2,1792]{1,0:T(2,128)S(1)} %get-tuple-element.30, ...), kind=kLoop, calls=%fused_computation.14 | loop fusion | flops 58720256 | bytes 117497856 | tf_op jit(solution)/shard_map/stack | solution.py:58
  319.9 20.6 %pad_maximum_fusion = bf16[4,1,2,1024,1792]{4,3,2,1,0:T(8,128)(2,1)} fusion(bf16[1,1,2,1024,1792]{4,3,2,1,0:T(8,128)(2,1)} %get-tuple-element.15, bf16[1,1,2,1024,1792]{4,3,2,1,0:T(8,128)(2,1)} %get-tuple-element.17, bf16[1,1,2,1024,1792]{4,3,2,1,0:T(8,128)(2,1)} %get-tuple-element.16, bf16[1,1,2,1024,1792]{4,3,2,1,0:T(8,128)(2,1)} %get-tuple-element.14), kind=kLoop, calls=%fused_computation | loop fusion | flops 44040192 | bytes 58720256 | tf_op jit(solution)/shard_map/stack | solution.py:58
  (24 shorter events, 1.9 us)
Async XLA Ops:
  7.2 242.0 %all-reduce.3.cloned.1.call-start = ((), (), s32[]{:S(2)}) async-start(), calls=%async_computation | async-start | bytes 131072 | tf_op jit(solution)/shard_map/psum | solution.py:21
  59.0 7.3 %copy-start = (bf16[4,1,448,16]{2,3,1,0:T(8,128)(2,1)S(1)}, bf16[4,1,448,16]{2,3,1,0:T(8,128)(2,1)}, u32[]{:S(2)}) copy-start(bf16[4,1,448,16]{2,3,1,0:T(8,128)(2,1)} %param.13) | copy-start | bytes 172036
  136.2 10.2 %copy-start.2 = (bf16[4,1,4,512]{3,2,1,0:T(4,128)(2,1)S(1)}, bf16[4,1,4,512]{3,2,1,0:T(4,128)(2,1)}, u32[]{:S(2)}) copy-start(bf16[4,1,4,512]{3,2,1,0:T(4,128)(2,1)} %param.14) | copy-start | bytes 49156
  187.8 61.4 %copy-start.7 = (f32[4,1,512]{2,1,0:T(1,128)S(1)}, f32[4,1,512]{2,1,0:T(1,128)}, u32[]{:S(2)}) copy-start(f32[4,1,512]{2,1,0:T(1,128)} %param.15) | copy-start | bytes 24580
  269.2 11.8 %copy-start.1 = (f32[4,1,2,1792]{3,2,1,0:T(2,128)S(1)}, f32[4,1,2,1792]{3,2,1,0:T(2,128)}, u32[]{:S(2)}) copy-start(f32[4,1,2,1792]{3,2,1,0:T(2,128)} %param.11) | copy-start | bytes 172036
  269.2 11.8 %copy-start.3 = (f32[1,2,1792]{2,1,0:T(2,128)S(1)}, f32[1,2,1792]{2,1,0:T(2,128)}, u32[]{:S(2)}) copy-start(f32[1,2,1792]{2,1,0:T(2,128)} %get-tuple-element.6) | copy-start | bytes 43012
  269.3 11.8 %copy-start.4 = (f32[1,2,1792]{2,1,0:T(2,128)S(1)}, f32[1,2,1792]{2,1,0:T(2,128)}, u32[]{:S(2)}) copy-start(f32[1,2,1792]{2,1,0:T(2,128)} %get-tuple-element.7) | copy-start | bytes 43012
  269.3 11.8 %copy-start.5 = (f32[1,2,1792]{2,1,0:T(2,128)S(1)}, f32[1,2,1792]{2,1,0:T(2,128)}, u32[]{:S(2)}) copy-start(f32[1,2,1792]{2,1,0:T(2,128)} %get-tuple-element.8) | copy-start | bytes 43012
  269.3 11.8 %copy-start.6 = (f32[1,2,1792]{2,1,0:T(2,128)S(1)}, f32[1,2,1792]{2,1,0:T(2,128)}, u32[]{:S(2)}) copy-start(f32[1,2,1792]{2,1,0:T(2,128)} %get-tuple-element.9) | copy-start | bytes 43012
Sparse Core Ops, SparseCore 0:
  218.7 30.3 all-reduce.2
where the time goes:
time: 348 us; the launch traced here: 347 us
  blocking collectives  110 us (32%)
  other arithmetic  91.3 us (26%)
  matrix products  80 us (23%)
  waiting for transfers between devices  30.6 us (9%)
  local copies, waits for them, and re-layouts  21.2 us (6%)
  between operations  14.2 us (4%)
    another operation x5, other arithmetic, shards(): return (jnp.stack(inner_outputs), jnp.stack(outer_outputs))  90.5 us
    dot_general x8, matrix products, combine_tile(): jnp.einsum('...ik,...kj->...ij', left, right, preferred_element_type=jnp....  80 us
    all_gather x1, blocking collectives, shards(): lax.all_gather(outer_left, 'col', axis=2, tiled=True)  69.6 us
    psum x1, waiting for transfers between devices, merge_layer(): inner_totals, outer_totals = lax.psum((inner_squares, outer_squares), 'row')  30.6 us
    all_gather x1, blocking collectives, shards(): lax.all_gather(inner_left, 'col', axis=3, tiled=True)  27 us
    unnamed x23, local copies, waits for them, and re-layouts  13.8 us
    all_gather x1, blocking collectives, shards(): lax.all_gather(inner_right, 'row', axis=3, tiled=True)  8.32 us
  transfers between devices with their start and end apart: 1, of which 1 were waited for; matrix products, arithmetic and copies ran while one was open for 0% of the time, Pallas kernels for 0%

commit v1 on v0

--- a/solution.py
+++ b/solution.py
@@ -36,7 +36,7 @@
     outer_outputs = []
     inner_rows, outer_rows = (
         lax.all_gather(inner_left, "col", axis=3, tiled=True),
-        lax.all_gather(outer_left, "col", axis=2, tiled=True),
+        jnp.concatenate(lax.all_gather(outer_left, "col"), axis=2),
     )
     inner_ranks, outer_ranks = (
         lax.all_gather(inner_right, "row", axis=3, tiled=True),

time: 348 us -> 292 us (0.84)
  blocking collectives: 110 us -> 72.1 us
  local copies, waits for them, and re-layouts: 21.2 us -> 2.71 us
    all_gather x1, blocking collectives: 69.6 us -> 31.4 us  [shards(): lax.all_gather(outer_left, 'col')]
    unnamed x23 -> x18, local copies, waits for them, and re-layouts: 13.8 us -> 0.98 us
    slice x1, local copies, waits for them, and re-layouts: 6.69 us -> 0.04 us  [shards(): outer_rows[layer_index]]
where the time goes in v1:
time: 292 us; the launch traced here: 291 us
  other arithmetic  91.1 us (31%)
  matrix products  80.2 us (27%)
  blocking collectives  72.1 us (25%)
  waiting for transfers between devices  31.1 us (11%)
  between operations  14.2 us (5%)
    another operation x5, other arithmetic, shards(): return (jnp.stack(inner_outputs), jnp.stack(outer_outputs))  90.3 us
    dot_general x8, matrix products, combine_tile(): jnp.einsum('...ik,...kj->...ij', left, right, preferred_element_type=jnp....  80.2 us
    all_gather x1, blocking collectives, shards(): lax.all_gather(outer_left, 'col')  31.4 us
    psum x1, waiting for transfers between devices, merge_layer(): inner_totals, outer_totals = lax.psum((inner_squares, outer_squares), 'row')  31 us
    all_gather x1, blocking collectives, shards(): lax.all_gather(inner_left, 'col', axis=3, tiled=True)  27 us
    all_gather x1, blocking collectives, shards(): lax.all_gather(inner_right, 'row', axis=3, tiled=True)  8.32 us
  transfers between devices with their start and end apart: 1, of which 1 were waited for; matrix products, arithmetic and copies ran while one was open for 0% of the time, Pallas kernels for 0%

profile of v1, /device:TPU:0, one launch (start us, length us, event | category | flops | bytes accessed | tf_op | source)
XLA Modules:
  0.0 291.4 jit_solution(8744202017365214063)
XLA Ops:
  7.2 0.9 copy.18
  8.2 8.3 %all_gather.16 = bf16[4,1,2,16,1792]{4,0,2,1,3:T(4,128)(2,1)S(1)} all-gather(bf16[4,1,2,4,1792]{4,0,2,1,3:T(4,128)(2,1)S(1)} %copy.18), channel_id=1, replica_groups=mesh['row'=4,'col'=8] {'row'}, dimensions={3}, use_global_device_ids=true | all-gather | bytes 573440 | tf_op jit(solution)/shard_map/all_gather | solution.py:42
  16.5 0.7 fusion.17
  17.1 27.0 %all_gather.15 = bf16[4,1,2,1024,16]{3,4,2,1,0:T(8,128)(2,1)S(1)} all-gather(bf16[4,1,2,128,16]{3,4,2,1,0:T(8,128)(2,1)} %param.9), channel_id=1, replica_groups=mesh['row'=4,'col'=8] {'col'}, dimensions={3}, use_global_device_ids=true | all-gather | bytes 294912 | tf_op jit(solution)/shard_map/all_gather | solution.py:38
  44.1 7.6 %fusion.10 = f32[2,1024,1792]{2,1,0:T(8,128)} fusion(bf16[1,1,2,16,1792]{4,0,2,1,3:T(2,128)(2,1)S(1)} %get-tuple-element.23, bf16[4,1,2,1024,16]{3,4,2,1,0:T(8,128)(2,1)S(1)} %all_gather.15), kind=kOutput, calls=%fused_computation.40 | convolution fusion | flops 117440512 | bytes 14974976 | tf_op jit(solution)/shard_map/...ik,...kj->...ij/dot_general | solution.py:10
  51.7 7.3 %fusion.8 = f32[2,1024,1792]{2,1,0:T(8,128)} fusion(bf16[1,1,2,16,1792]{4,0,2,1,3:T(2,128)(2,1)S(1)} %get-tuple-element.25, bf16[4,1,2,1024,16]{3,4,2,1,0:T(8,128)(2,1)S(1)} %all_gather.15), kind=kOutput, calls=%fused_computation.36 | convolution fusion | flops 117440512 | bytes 14974976 | tf_op jit(solution)/shard_map/...ik,...kj->...ij/dot_general | solution.py:10
  59.0 7.3 %fusion.9 = f32[2,1024,1792]{2,1,0:T(8,128)} fusion(bf16[1,1,2,16,1792]{4,0,2,1,3:T(2,128)(2,1)S(1)} %get-tuple-element.22, bf16[4,1,2,1024,16]{3,4,2,1,0:T(8,128)(2,1)S(1)} %all_gather.15), kind=kOutput, calls=%fused_computation.38 | convolution fusion | flops 117440512 | bytes 14974976 | tf_op jit(solution)/shard_map/...ik,...kj->...ij/dot_general | solution.py:10
  66.3 31.4 %all-gather = bf16[32,1,448,16]{2,3,1,0:T(8,128)(2,1)S(1)} all-gather(bf16[4,1,448,16]{2,3,1,0:T(8,128)(2,1)S(1)} %copy-done), channel_id=2, replica_groups=mesh['row'=4,'col'=8] {'col'}, dimensions={0}, use_global_device_ids=true | all-gather | bytes 516096 | tf_op jit(solution)/shard_map/all_gather | solution.py:39
  97.7 0.3 copy.64
  98.0 0.2 reshape.201
  98.2 5.4 %all_gather.19 = bf16[4,1,16,512]{3,0,1,2:T(4,128)(2,1)S(1)} all-gather(bf16[4,1,4,512]{3,0,1,2:T(4,128)(2,1)S(1)} %copy.24), channel_id=1, replica_groups=mesh['row'=4,'col'=8] {'row'}, dimensions={2}, use_global_device_ids=true | all-gather | bytes 81920 | tf_op jit(solution)/shard_map/all_gather | solution.py:43
  103.9 0.2 reshape.205
  104.2 6.7 %multiply_reduce_fusion.7 = (f32[512]{0:T(512)}, f32[3584,512]{1,0:T(8,128)}) fusion(bf16[3584,16]{0,1:T(8,128)(2,1)S(1)} %reshape.201, bf16[1,1,16,512]{3,0,1,2:T(2,128)(2,1)S(1)} %get-tuple-element.26, bf16[4,1,3584,512]{3,2,1,0:T(8,128)(2,1)} %param.12), kind=kOutput, calls=%fused_computation.29 | convolution fusion | flops 66059776 | bytes 11143168 | tf_op jit(solution)/shard_map/...ik,...kj->...ij/dot_general | solution.py:10
  110.9 6.8 %multiply_reduce_fusion.6 = (f32[512]{0:T(512)}, f32[3584,512]{1,0:T(8,128)}) fusion(bf16[3584,16]{0,1:T(8,128)(2,1)S(1)} %reshape.203, bf16[1,1,16,512]{3,0,1,2:T(2,128)(2,1)S(1)} %get-tuple-element.28, bf16[4,1,3584,512]{3,2,1,0:T(8,128)(2,1)} %param.12), kind=kOutput, calls=%fused_computation.27 | convolution fusion | flops 66059776 | bytes 11143168 | tf_op jit(solution)/shard_map/...ik,...kj->...ij/dot_general | solution.py:10
  117.7 6.8 %multiply_reduce_fusion.5 = (f32[512]{0:T(512)}, f32[3584,512]{1,0:T(8,128)}) fusion(bf16[3584,16]{0,1:T(8,128)(2,1)S(1)} %reshape.205, bf16[1,1,16,512]{3,0,1,2:T(2,128)(2,1)S(1)} %get-tuple-element.27, bf16[4,1,3584,512]{3,2,1,0:T(8,128)(2,1)} %param.12), kind=kOutput, calls=%fused_computation.25 | convolution fusion | flops 66059776 | bytes 11143168 | tf_op jit(solution)/shard_map/...ik,...kj->...ij/dot_general | solution.py:10
  124.5 6.8 %multiply_reduce_fusion.4 = (f32[512]{0:T(512)}, f32[3584,512]{1,0:T(8,128)}) fusion(bf16[3584,16]{0,1:T(8,128)(2,1)S(1)} %reshape.207, bf16[1,1,16,512]{3,0,1,2:T(2,128)(2,1)S(1)} %get-tuple-element.29, bf16[4,1,3584,512]{3,2,1,0:T(8,128)(2,1)} %param.12), kind=kOutput, calls=%fused_computation.23 | convolution fusion | flops 66059776 | bytes 11143168 | tf_op jit(solution)/shard_map/...ik,...kj->...ij/dot_general | solution.py:10
  131.3 31.0 %multiply_reduce_fusion.3 = (f32[2,1792]{1,0:T(2,128)}, f32[2,1792]{1,0:T(2,128)}, f32[2,1792]{1,0:T(2,128)}, f32[2,1792]{1,0:T(2,128)}, f32[2,1024,1792]{2,1,0:T(8,128)}) fusion(bf16[4,1,2,1024,1792]{4,3,2,1,0:T(8,128)(2,1)} %param.8, f32[2,1024,1792]{2,1,0:T(8,128)} %fusion.10, f32[2,1024,1792]{2,1,0:T(8,128)} %fusion.8, f32[2,1024,1792]{2,1,0:T(8,128)} %fusion.9, ...), kind=kOutput, calls=%fused_computation.13 | convolution fusion | flops 176146432 | bytes 88432640 | tf_op jit(solution)/shard_map/...ik,...kj->...ij/dot_general | solution.py:10
  162.3 31.0 %all-reduce.3.cloned.1.call-done = (f32[1,2,1792]{2,1,0:T(2,128)}, f32[1,2,1792]{2,1,0:T(2,128)}, f32[1,2,1792]{2,1,0:T(2,128)}, f32[1,2,1792]{2,1,0:T(2,128)}, ...) async-done(((f32[1,2,1792]{2,1,0:T(2,128)}, f32[1,2,1792]{2,1,0:T(2,128)}, f32[1,2,1792]{2,1,0:T(2,128)}, f32[1,2,1792]{2,1,0:T(2,128)}, ...) | async-done | bytes 65552 | tf_op jit(solution)/shard_map/psum | solution.py:21
  193.3 0.7 bitcast_multiply_fusion.7
  194.0 9.1 %fusion.4 = (bf16[1,1,3584,512]{3,2,1,0:T(8,128)(2,1)S(1)}, bf16[1,1,3584,512]{3,2,1,0:T(8,128)(2,1)}) fusion(f32[3584,512]{1,0:T(8,128)} %get-tuple-element.46, f32[512]{0:T(512)S(1)} %bitcast.172, f32[3584,512]{1,0:T(8,128)} %get-tuple-element.44, f32[512]{0:T(512)S(1)} %bitcast.173), kind=kLoop, calls=%fused_computation.30 | loop fusion | flops 7340032 | bytes 22024192 | tf_op jit(solution)/shard_map/stack | solution.py:58
  203.2 10.2 %fusion.6 = (bf16[1,1,3584,512]{3,2,1,0:T(8,128)(2,1)}, bf16[1,1,3584,512]{3,2,1,0:T(8,128)(2,1)}) fusion(f32[3584,512]{1,0:T(8,128)} %get-tuple-element.42, f32[512]{0:T(512)S(1)} %bitcast.171, f32[3584,512]{1,0:T(8,128)} %get-tuple-element.40, f32[512]{0:T(512)S(1)} %bitcast.170), kind=kLoop, calls=%fused_computation.32 | loop fusion | flops 7340032 | bytes 22024192 | tf_op jit(solution)/shard_map/stack | solution.py:58
  213.4 11.6 %pad_maximum_fusion.1 = bf16[4,1,3584,512]{3,2,1,0:T(8,128)(2,1)} fusion(bf16[1,1,3584,512]{3,2,1,0:T(8,128)(2,1)} %get-tuple-element.50, bf16[1,1,3584,512]{3,2,1,0:T(8,128)(2,1)} %get-tuple-element.49, bf16[1,1,3584,512]{3,2,1,0:T(8,128)(2,1)} %get-tuple-element.48, bf16[1,1,3584,512]{3,2,1,0:T(8,128)(2,1)S(1)} %get-tuple-element.47), kind=kLoop, calls=%fused_computation.1 | loop fusion | flops 22020096 | bytes 29360128 | tf_op jit(solution)/shard_map/stack | solution.py:58
  225.1 38.7 %fusion = (bf16[1,1,2,1024,1792]{4,3,2,1,0:T(8,128)(2,1)}, bf16[1,1,2,1024,1792]{4,3,2,1,0:T(8,128)(2,1)}, bf16[1,1,2,1024,1792]{4,3,2,1,0:T(8,128)(2,1)}, bf16[1,1,2,1024,1792]{4,3,2,1,0:T(8,128)(2,1)}) fusion(f32[2,1024,1792]{2,1,0:T(8,128)} %get-tuple-element.38, f32[2,1792]{1,0:T(2,128)S(1)} %get-tuple-element.30, ...), kind=kLoop, calls=%fused_computation.14 | loop fusion | flops 58720256 | bytes 117497856 | tf_op jit(solution)/shard_map/stack | solution.py:58
  263.9 20.6 %pad_maximum_fusion = bf16[4,1,2,1024,1792]{4,3,2,1,0:T(8,128)(2,1)} fusion(bf16[1,1,2,1024,1792]{4,3,2,1,0:T(8,128)(2,1)} %get-tuple-element.15, bf16[1,1,2,1024,1792]{4,3,2,1,0:T(8,128)(2,1)} %get-tuple-element.17, bf16[1,1,2,1024,1792]{4,3,2,1,0:T(8,128)(2,1)} %get-tuple-element.16, bf16[1,1,2,1024,1792]{4,3,2,1,0:T(8,128)(2,1)} %get-tuple-element.14), kind=kLoop, calls=%fused_computation | loop fusion | flops 44040192 | bytes 58720256 | tf_op jit(solution)/shard_map/stack | solution.py:58
  (24 shorter events, 0.6 us)
Async XLA Ops:
  7.2 186.2 %all-reduce.3.cloned.1.call-start = ((), (), s32[]{:S(2)}) async-start(), calls=%async_computation | async-start | bytes 131072 | tf_op jit(solution)/shard_map/psum | solution.py:21
  59.0 7.3 %copy-start = (bf16[4,1,448,16]{2,3,1,0:T(8,128)(2,1)S(1)}, bf16[4,1,448,16]{2,3,1,0:T(8,128)(2,1)}, u32[]{:S(2)}) copy-start(bf16[4,1,448,16]{2,3,1,0:T(8,128)(2,1)} %param.13) | copy-start | bytes 172036
  59.0 39.2 %copy-start.2 = (bf16[4,1,4,512]{3,2,1,0:T(4,128)(2,1)S(1)}, bf16[4,1,4,512]{3,2,1,0:T(4,128)(2,1)}, u32[]{:S(2)}) copy-start(bf16[4,1,4,512]{3,2,1,0:T(4,128)(2,1)} %param.14) | copy-start | bytes 49156
  131.3 62.0 %copy-start.7 = (f32[4,1,512]{2,1,0:T(1,128)S(1)}, f32[4,1,512]{2,1,0:T(1,128)}, u32[]{:S(2)}) copy-start(f32[4,1,512]{2,1,0:T(1,128)} %param.15) | copy-start | bytes 24580
  213.4 11.7 %copy-start.1 = (f32[4,1,2,1792]{3,2,1,0:T(2,128)S(1)}, f32[4,1,2,1792]{3,2,1,0:T(2,128)}, u32[]{:S(2)}) copy-start(f32[4,1,2,1792]{3,2,1,0:T(2,128)} %param.11) | copy-start | bytes 172036
  213.4 11.7 %copy-start.3 = (f32[1,2,1792]{2,1,0:T(2,128)S(1)}, f32[1,2,1792]{2,1,0:T(2,128)}, u32[]{:S(2)}) copy-start(f32[1,2,1792]{2,1,0:T(2,128)} %get-tuple-element.6) | copy-start | bytes 43012
  213.4 11.7 %copy-start.4 = (f32[1,2,1792]{2,1,0:T(2,128)S(1)}, f32[1,2,1792]{2,1,0:T(2,128)}, u32[]{:S(2)}) copy-start(f32[1,2,1792]{2,1,0:T(2,128)} %get-tuple-element.7) | copy-start | bytes 43012
  213.4 11.7 %copy-start.5 = (f32[1,2,1792]{2,1,0:T(2,128)S(1)}, f32[1,2,1792]{2,1,0:T(2,128)}, u32[]{:S(2)}) copy-start(f32[1,2,1792]{2,1,0:T(2,128)} %get-tuple-element.8) | copy-start | bytes 43012
  213.4 11.7 %copy-start.6 = (f32[1,2,1792]{2,1,0:T(2,128)S(1)}, f32[1,2,1792]{2,1,0:T(2,128)}, u32[]{:S(2)}) copy-start(f32[1,2,1792]{2,1,0:T(2,128)} %get-tuple-element.9) | copy-start | bytes 43012
Sparse Core Ops, SparseCore 0:
  162.4 30.8 all-reduce.2
